TPU v7x, 8 devices: a whole 2x2x1 slice. The times are simulated.
8 devices in a mesh: dp: 1 (over z), tp: 2 (over y), sp: 4 (over x, core).
Axes of the slice: x: 2, y: 2, z: 1, core: 2. Of those that a mesh axis runs over, the one named last changes fastest.
Arguments:
- hidden: bfloat16 [96, 16384], P('dp')
- lengths: int32 [96], P('dp')
- k_cache: bfloat16 [96, 512, 8, 128], P('dp', 'sp', 'tp')
- v_cache: bfloat16 [96, 512, 8, 128], P('dp', 'sp', 'tp')
- norm_gain: bfloat16 [16384], replicated
- w_q: bfloat16 [16384, 16384], P(None, 'tp')
- w_k: bfloat16 [16384, 1024], P(None, 'tp')
- w_v: bfloat16 [16384, 1024], P(None, 'tp')
- w_o: bfloat16 [16384, 16384], P('tp')
- inv_freq: float32 [64], replicated
Outputs:
- output 1: bfloat16 [96, 16384], P('dp')
- output 2: bfloat16 [96, 512, 8, 128], P('dp', 'sp', 'tp')
- output 3: bfloat16 [96, 512, 8, 128], P('dp', 'sp', 'tp')
All inputs are finite; a program needn't handle non-finite values.
Results may differ from a plain program's by a relative error of at most 0.0088644.
Values sent between devices are 32-bit elements.
A program may use at most 2.5 GiB of HBM per device.

v0:
```python
import jax
import jax.numpy as jnp
from jax import lax
from jax.sharding import PartitionSpec as P

NORM_EPS = 1e-5
NEG_BIG = -1e30


def rms_norm(hidden, norm_gain):
    hidden_f32 = hidden.astype(jnp.float32)
    inv_rms = lax.rsqrt(jnp.mean(hidden_f32 * hidden_f32, axis=-1, keepdims=True) + NORM_EPS)
    return (hidden_f32 * inv_rms * norm_gain.astype(jnp.float32)).astype(jnp.bfloat16)


def apply_rope(head_vec, angles):
    half_dim = head_vec.shape[-1] // 2
    vec_f32 = head_vec.astype(jnp.float32)
    cos_ang = jnp.cos(angles)[:, None, :]
    sin_ang = jnp.sin(angles)[:, None, :]
    lo_half = vec_f32[..., :half_dim]
    hi_half = vec_f32[..., half_dim:]
    rotated = jnp.concatenate([lo_half * cos_ang - hi_half * sin_ang, hi_half * cos_ang + lo_half * sin_ang], axis=-1)
    return rotated.astype(jnp.bfloat16)


def project_new_token(hidden, lengths, norm_gain, w_q, w_k, w_v, inv_freq):
    batch_size = hidden.shape[0]
    head_dim = 2 * inv_freq.shape[0]
    normed = rms_norm(hidden, norm_gain)
    q_heads = jnp.dot(normed, w_q, preferred_element_type=jnp.float32).astype(jnp.bfloat16).reshape(batch_size, -1, head_dim)
    k_new = jnp.dot(normed, w_k, preferred_element_type=jnp.float32).astype(jnp.bfloat16).reshape(batch_size, -1, head_dim)
    v_new = jnp.dot(normed, w_v, preferred_element_type=jnp.float32).astype(jnp.bfloat16).reshape(batch_size, -1, head_dim)
    angles = lengths.astype(jnp.float32)[:, None] * inv_freq[None, :]
    return apply_rope(q_heads, angles), apply_rope(k_new, angles), v_new


def write_and_attend(q_rot, k_rot, v_new, lengths, k_cache, v_cache):
    batch_size, slot_count, kv_local, head_dim = k_cache.shape
    slot_start = lax.axis_index('sp') * slot_count
    local_pos = lengths - slot_start
    owned = (local_pos >= 0) & (local_pos < slot_count)
    write_pos = jnp.where(owned, local_pos, slot_count)
    row_ids = jnp.arange(batch_size)
    k_upd = k_cache.at[row_ids, write_pos].set(k_rot, mode='drop')
    v_upd = v_cache.at[row_ids, write_pos].set(v_new, mode='drop')
    group_size = q_rot.shape[1] // kv_local
    q_grp = q_rot.reshape(batch_size, kv_local, group_size, head_dim)
    scores = jnp.einsum('bkgd,bskd->bkgs', q_grp, k_upd, preferred_element_type=jnp.float32) * head_dim ** -0.5
    valid_mask = ((slot_start + jnp.arange(slot_count))[None, :] <= lengths[:, None])[:, None, None, :]
    scores = jnp.where(valid_mask, scores, NEG_BIG)
    part_max = jnp.max(scores, axis=-1)
    weights = jnp.where(valid_mask, jnp.exp(scores - part_max[..., None]), 0.0)
    part_sum = jnp.sum(weights, axis=-1)
    part_out = jnp.einsum('bkgs,bskd->bkgd', weights.astype(jnp.bfloat16), v_upd, preferred_element_type=jnp.float32)
    return k_upd, v_upd, part_max, part_sum, part_out


def device_step(hidden, lengths, k_cache, v_cache, norm_gain, w_q, w_k, w_v, w_o, inv_freq):
    batch_size = hidden.shape[0]
    q_rot, k_rot, v_new = project_new_token(hidden, lengths, norm_gain, w_q, w_k, w_v, inv_freq)
    k_upd, v_upd, part_max, part_sum, part_out = write_and_attend(q_rot, k_rot, v_new, lengths, k_cache, v_cache)
    all_max = lax.all_gather(part_max, 'sp')
    all_sum = lax.all_gather(part_sum, 'sp')
    all_out = lax.all_gather(part_out, 'sp')
    top_score = jnp.max(all_max, axis=0)
    factor = jnp.exp(all_max - top_score[None])
    weighted = jnp.sum(factor[..., None] * all_out, axis=0)
    weight_sum = jnp.sum(factor * all_sum, axis=0)
    attn_out = (weighted / weight_sum[..., None]).astype(jnp.bfloat16).reshape(batch_size, -1)
    proj_out = lax.psum(jnp.dot(attn_out, w_o, preferred_element_type=jnp.float32), 'tp')
    y_out = (hidden.astype(jnp.float32) + proj_out).astype(jnp.bfloat16)
    return y_out, k_upd, v_upd


def solution(mesh):
    cache_spec = P('dp', 'sp', 'tp', None)
    in_specs = (P('dp', None), P('dp'), cache_spec, cache_spec, P(None), P(None, 'tp'), P(None, 'tp'), P(None, 'tp'), P('tp', None), P(None))
    out_specs = (P('dp', None), cache_spec, cache_spec)
    return jax.shard_map(device_step, mesh=mesh, in_specs=in_specs, out_specs=out_specs, check_vma=False)
```

profile of v0, /device:TPU:0, one launch (start us, length us, event | category | flops | bytes accessed | tf_op | source)
XLA Modules:
  0.0 534.1 jit_solution(9920731723092012745)
XLA Ops:
  7.2 0.0 all-gather.5.cloned.1.call-start
  7.2 12.5 %copy.34 = bf16[96,128,4,128]{3,2,1,0:T(4,128)(2,1)} copy(bf16[96,128,4,128]{3,2,1,0:T(4,128)(2,1)} %param.12) | data formatting | bytes 25165824
  19.8 5.3 copy.35
  25.1 0.7 fusion.5
  25.8 0.1 broadcast_compare_fusion
  25.9 8.6 %convolution_convert_fusion.1 = bf16[96,512]{1,0:T(8,128)(2,1)S(1)} fusion(bf16[16384,512]{1,0:T(8,128)(2,1)} %param.17, bf16[96,16384]{1,0:T(8,128)(2,1)S(1)} %copy-done, f32[16384]{0:T(1024)S(1)} %convert_element_type.51, f32[96]{0:T(128)S(1)} %add_rsqrt_fusion), kind=kOutput, calls=%fused_computation.36 | convolution fusion | flops 1616953344 | bytes 20087168 | tf_op jit(solution)/shard_map/dot_general | solution.py:33
  34.6 9.3 %fusion.25 = f32[96,512]{1,0:T(8,128)} fusion(bf16[16384,512]{1,0:T(8,128)(2,1)} %param.16, bf16[96,16384]{1,0:T(8,128)(2,1)S(1)} %copy-done, f32[16384]{0:T(1024)S(1)} %convert_element_type.51, f32[96]{0:T(128)S(1)} %add_rsqrt_fusion), kind=kOutput, calls=%fused_computation.38 | convolution fusion | flops 1617002496 | bytes 20185472 | tf_op jit(solution)/shard_map/dot_general | solution.py:32
  43.9 1.0 reshape.110
  44.9 85.7 %fusion.12 = f32[12,8,64,128]{3,1,2,0:T(8,128)} fusion(bf16[16384,8192]{1,0:T(8,128)(2,1)} %param.15, bf16[96,16384]{1,0:T(8,128)(2,1)S(1)} %copy-done, f32[16384]{0:T(1024)S(1)} %convert_element_type.51, f32[96]{0:T(128)S(1)} %add_rsqrt_fusion), kind=kOutput, calls=%fused_computation.24 | convolution fusion | flops 25777668096 | bytes 274792832 | tf_op jit(solution)/shard_map/dot_general | solution.py:31
  130.6 2.4 copy.17
  133.1 0.2 multiply_cosine_fusion
  133.3 0.2 subtract_convert_fusion.1
  133.5 3.0 subtract_convert_fusion
  136.5 0.1 pad_maximum_fusion
  136.6 13.8 %scatter_fusion = bf16[96,128,4,128]{3,2,1,0:T(4,128)(2,1)} fusion(bf16[96,128,4,128]{3,2,1,0:T(4,128)(2,1)} %copy.34, s32[96]{0:T(128)S(1)} %fusion.28, bf16[96,4,128]{2,1,0:T(4,128)(2,1)S(1)} %pad_maximum_fusion), kind=kCustom, calls=%fused_computation | custom fusion | bytes 295680 | tf_op jit(solution)/shard_map/scatter | solution.py:45
  150.4 13.6 %scatter_fusion.1 = bf16[96,128,4,128]{3,2,1,0:T(4,128)(2,1)} fusion(bf16[96,128,4,128]{3,2,1,0:T(4,128)(2,1)} %copy.35, s32[96]{0:T(128)S(1)} %fusion.28, bf16[96,4,128]{2,1,0:T(4,128)(2,1)S(1)} %reshape.119), kind=kCustom, calls=%fused_computation.1 | custom fusion | bytes 295680 | tf_op jit(solution)/shard_map/scatter | solution.py:46
  164.0 14.1 %fusion.9 = (f32[96,4,16]{2,1,0:T(4,128)S(1)}, f32[96,4,16,128]{3,2,1,0:T(8,128)}) fusion(pred[96,128]{1,0:T(8,128)(4,1)S(1)} %broadcast_compare_fusion, bf16[96,128,4,128]{3,2,1,0:T(4,128)(2,1)} %scatter_fusion, bf16[96,4,16,64]{3,2,1,0:T(8,128)(2,1)} %bitcast.33, bf16[96,4,16,64]{3,2,1,0:T(8,128)(2,1)} %bitcast.32), kind=kOutput, calls=%fused_computation.21 | convolution fusion | flops 206825472 | bytes 17338368 | tf_op jit(solution)/shard_map/bkgd,bskd->bkgs/dot_general | solution.py:49
  178.2 10.7 %fusion = f32[96,4,16,128]{3,2,1,0:T(8,128)} fusion(bf16[96,128,4,128]{3,2,1,0:T(4,128)(2,1)} %scatter_fusion.1, f32[96,4,16,128]{3,2,1,0:T(8,128)} %get-tuple-element.12, f32[96,4,16]{2,1,0:T(4,128)S(1)} %get-tuple-element.11, pred[96,128]{1,0:T(8,128)(4,1)S(1)} %broadcast_compare_fusion), kind=kOutput, calls=%fused_computation.2 | convolution fusion | flops 205258752 | bytes 18911232 | tf_op jit(solution)/shard_map/bkgs,bskd->bkgd/dot_general | solution.py:55
  188.8 0.0 all-gather.5.cloned.1.call-update
  188.8 0.0 all-reduce.2.cloned.1.call-start
  188.9 13.9 %all-gather = f32[384,4,16]{2,1,0:T(4,128)} all-gather(f32[96,4,16]{2,1,0:T(4,128)S(1)} %get-tuple-element.11), channel_id=2, replica_groups=mesh['dp'=1,'tp'=2,'sp'=4] {'sp'}, dimensions={0}, use_global_device_ids=true | all-gather | bytes 122880 | tf_op jit(solution)/shard_map/all_gather | solution.py:63
  202.8 1.4 reduce_max.19
  204.2 3.4 fusion.10
  207.5 19.9 %all-gather.2 = f32[384,4,16]{2,1,0:T(4,128)S(1)} all-gather(f32[96,4,16]{2,1,0:T(4,128)S(1)} %fusion.10), channel_id=4, replica_groups=mesh['dp'=1,'tp'=2,'sp'=4] {'sp'}, dimensions={0}, use_global_device_ids=true | all-gather | bytes 122880 | tf_op jit(solution)/shard_map/all_gather | solution.py:64
  227.5 1.3 multiply_reduce_fusion.1
  228.8 50.1 %all-gather.5.cloned.1.call-done = f32[384,4,16,128]{3,2,1,0:T(8,128)} async-done(((f32[96,4,16,128]{3,2,1,0:T(8,128)}), f32[384,4,16,128]{3,2,1,0:T(8,128)}) %all-gather.5.cloned.1.call-update) | async-done | bytes 12582928 | tf_op jit(solution)/shard_map/all_gather | solution.py:65
  278.9 7.9 %multiply_reduce_fusion = f32[96,4,16,128]{3,2,1,0:T(8,128)S(1)} fusion(f32[4,96,4,16,128]{4,3,2,1,0:T(8,128)} %bitcast.28, f32[4,96,4,16]{3,2,1,0:T(4,128)} %get-tuple-element.4), kind=kLoop, calls=%fused_computation.6 | loop fusion | flops 5505024 | bytes 15826944 | tf_op jit(solution)/shard_map/reduce_sum | solution.py:68
  286.8 1.9 divide_convert_fusion
  288.7 85.5 %fusion.14 = f32[96,16384]{1,0:T(8,128)} fusion(bf16[8192,16384]{1,0:T(8,128)(2,1)} %param.18, bf16[12,8,64,128]{3,2,1,0:T(8,128)(2,1)} %bitcast.31), kind=kOutput, calls=%fused_computation.25 | convolution fusion | flops 25769803776 | bytes 276299776 | tf_op jit(solution)/shard_map/dot_general | solution.py:71
  374.2 0.0 all-reduce.2.cloned.1.call-update
  374.2 148.0 %all-reduce.2.cloned.1.call-done = f32[96,16384]{1,0:T(8,128)} async-done(((f32[96,16384]{1,0:T(8,128)}), f32[96,16384]{1,0:T(8,128)}) %all-reduce.2.cloned.1.call-update) | async-done | bytes 6291472 | tf_op jit(solution)/shard_map/psum | solution.py:71
  522.2 5.0 fusion.8
  (18 shorter events, 0.1 us)
Async XLA Ops:
  7.2 271.7 %all-gather.5.cloned.1.call-start = ((), (), s32[]{:S(2)}) async-start(), calls=%async_computation.1 | async-start | bytes 15728640 | tf_op jit(solution)/shard_map/all_gather | solution.py:65
  7.2 12.5 %copy-start.1 = (bf16[96,128,4,128]{3,2,1,0:T(4,128)(2,1)S(1)}, bf16[96,128,4,128]{3,2,1,0:T(4,128)(2,1)}, u32[]{:S(2)}) copy-start(bf16[96,128,4,128]{3,2,1,0:T(4,128)(2,1)} %param.13) | copy-start | bytes 37748740
  19.8 5.3 copy-start.5
  19.8 5.3 %copy-start = (bf16[96,16384]{1,0:T(8,128)(2,1)S(1)}, bf16[96,16384]{1,0:T(8,128)(2,1)}, u32[]{:S(2)}) copy-start(bf16[96,16384]{1,0:T(8,128)(2,1)} %param.10) | copy-start | bytes 9437188
  25.1 0.9 copy-start.3
  130.6 2.5 copy-start.4
  188.8 333.3 %all-reduce.2.cloned.1.call-start = ((), (), s32[]{:S(2)}) async-start(), calls=%async_computation | async-start | bytes 12582912 | tf_op jit(solution)/shard_map/psum | solution.py:71
  204.2 23.3 %copy-start.2 = (f32[384,4,16]{2,1,0:T(4,128)S(1)}, f32[384,4,16]{2,1,0:T(4,128)}, u32[]{:S(2)}) copy-start(f32[384,4,16]{2,1,0:T(4,128)} %all-gather) | copy-start | bytes 294916
Sparse Core Ops, SparseCore 0:
  189.0 89.9 all-gather.4
  374.3 147.8 all-reduce.1
where the time goes:
time: 535 us; the launch traced here: 534 us
  matrix products  214 us (40%)
  waiting for transfers between devices  198 us (37%)
  local copies, waits for them, and re-layouts  48.7 us (9%)
  blocking collectives  33.8 us (6%)
  other arithmetic  25.2 us (5%)
  between operations  14.2 us (3%)
    psum x1, waiting for transfers between devices, device_step(): lax.psum(jnp.dot(attn_out, w_o, preferred_element_type=jnp.float32), 'tp')  148 us
    dot_general x1, matrix products, project_new_token(): jnp.dot(normed, w_q, preferred_element_type=jnp.float32)  85.7 us
    dot_general x1, matrix products, device_step(): jnp.dot(attn_out, w_o, preferred_element_type=jnp.float32)  85.5 us
    all_gather x1, waiting for transfers between devices, device_step(): all_out = lax.all_gather(part_out, 'sp')  50.1 us
    unnamed x15, local copies, waits for them, and re-layouts  20.3 us
    all_gather x1, blocking collectives, device_step(): all_sum = lax.all_gather(part_sum, 'sp')  19.9 us
    dot_general x1, matrix products, write_and_attend(): jnp.einsum('bkgd,bskd->bkgs', q_grp, k_upd, preferred_element_type=jnp.fl...  14.1 us
    all_gather x1, blocking collectives, device_step(): all_max = lax.all_gather(part_max, 'sp')  13.9 us
  transfers between devices with their start and end apart: 2, of which 2 were waited for; matrix products, arithmetic and copies ran while one was open for 1% of the time, Pallas kernels for 0%

commit v1 on v0

v1 whole, which is shorter than its diff:
```python
import functools

import jax
import jax.numpy as jnp
from jax import lax
from jax.experimental import pallas as pl
from jax.experimental.pallas import tpu as pltpu
from jax.sharding import PartitionSpec as P

NORM_EPS = 1e-5
HEAD = 128
KT = 2048
WIDE = 512
SLOTS = 12
MIB = 2 ** 20
MESH_ID = pl.DeviceIdType.MESH
SEQS = 8
RING = 8
AHEAD = 4
MASKED = -3e38
SCALE = HEAD ** -0.5
OUT_K = 4096
OUT_W = 512
OUT_SLOTS = 9
PIECE = 8


def rope(vec, cos_full, sin_signed):
    rounded = vec.astype(jnp.bfloat16).astype(jnp.float32)
    rotated = rounded * cos_full + pltpu.roll(rounded, 64, 1) * sin_signed
    return rotated.astype(jnp.bfloat16).astype(jnp.float32)


def qkv_kernel(len_ref, hid_hbm, gain_ref, freq_ref, wq, wk, wv, out_hbm,
               hid, normed, gain, trig, wbuf, acc, heads, hid_sem, w_sem, v_sem,
               x_send, x_recv, d_send, d_recv, f_send, f_recv, out_sem):
    batch, dim = hid.shape
    n_k = dim // KT
    n_head = heads.shape[1] - 2
    cols = n_head * HEAD
    n_wide = cols // WIDE - 1
    half = WIDE // 2
    t_wide = n_k
    t_tail = t_wide + n_wide * n_k
    t_end = t_tail + 2 * n_k
    s = lax.axis_index('sp')
    x_peer = lax.rem(s + 2, 4)
    d_peer = s + 1 - 2 * lax.rem(s, 2)

    units = [(0, 2)] + [(2 + 4 * u, 4) for u in range(n_wide)] + [(2 + 4 * n_wide, 2), (4 + 4 * n_wide, 2)]

    def slot_of(t):
        return lax.rem(t, SLOTS)

    def rows_of(k):
        return pl.ds(pl.multiple_of(k * KT, KT), KT)

    def kv_copies(t):
        lanes = pl.ds(pl.multiple_of(s * HEAD, HEAD), HEAD)
        slot = slot_of(t)
        return (pltpu.make_async_copy(wk.at[rows_of(t), lanes], wbuf.at[slot, :, pl.ds(0, HEAD)], w_sem.at[slot]),
                pltpu.make_async_copy(wv.at[rows_of(t), lanes], wbuf.at[slot, :, pl.ds(HEAD, HEAD)], v_sem.at[slot]))

    def wide_copy(t):
        i = t - t_wide
        lanes = pl.ds(pl.multiple_of(s * cols + lax.div(i, n_k) * WIDE, WIDE), WIDE)
        return pltpu.make_async_copy(wq.at[rows_of(lax.rem(i, n_k)), lanes], wbuf.at[slot_of(t)], w_sem.at[slot_of(t)])

    def tail_copy(t):
        i = t - t_tail
        lanes = pl.ds(pl.multiple_of(s * cols + n_wide * WIDE + lax.div(i, n_k) * half, half), half)
        return pltpu.make_async_copy(wq.at[rows_of(lax.rem(i, n_k)), lanes], wbuf.at[slot_of(t), :, pl.ds(0, half)], w_sem.at[slot_of(t)])

    def start_tile(t):
        @pl.when(t < t_tail)
        def _():
            wide_copy(t).start(priority=1)

        @pl.when((t >= t_tail) & (t < t_end))
        def _():
            tail_copy(t).start(priority=1)

    hid_copy = pltpu.make_async_copy(hid_hbm, hid, hid_sem)
    hid_copy.start()
    for t in range(n_k):
        for cp in kv_copies(t):
            cp.start(priority=1)
    for t in range(n_k, SLOTS):
        wide_copy(t).start(priority=1)

    barrier = pltpu.get_barrier_semaphore()
    for peer in (x_peer, d_peer):
        pl.semaphore_signal(barrier, inc=1, device_id={'sp': peer}, device_id_type=MESH_ID)
    pl.semaphore_wait(barrier, 2)

    freq = freq_ref[...]

    def angle_step(b, carry):
        trig[0, pl.ds(b, 1), :] = len_ref[b].astype(jnp.float32) * freq
        return carry

    lax.fori_loop(0, batch, angle_step, 0)
    angles = trig[0]
    sin_full = jnp.sin(angles)
    lane = lax.broadcasted_iota(jnp.int32, sin_full.shape, 1)
    trig[1] = jnp.where(lane < 64, -sin_full, sin_full)
    trig[0] = jnp.cos(angles)
    gain[...] = gain_ref[...].astype(jnp.float32)

    hid_copy.wait()
    step = 512

    def sq_step(i, acc):
        x = hid[:, pl.ds(pl.multiple_of(i * step, step), step)].astype(jnp.float32)
        x = x * x
        for t in range(step // 128):
            acc = acc + x[:, t * 128:(t + 1) * 128]
        return acc

    sq = lax.fori_loop(0, dim // step, sq_step, jnp.zeros((batch, 128), jnp.float32))
    inv = lax.rsqrt(jnp.sum(sq, axis=1, keepdims=True) / dim + NORM_EPS)
    inv = jnp.broadcast_to(inv, (batch, 128))

    def norm_step(i, carry):
        for t in range(step // 128):
            sl = pl.ds(pl.multiple_of(i * step + t * 128, 128), 128)
            x = hid[:, sl].astype(jnp.float32)
            row = gain[pl.ds(i * (step // 128) + t, 1), :]
            normed[:, sl] = (x * inv * row).astype(jnp.bfloat16)
        return carry

    lax.fori_loop(0, dim // step, norm_step, 0)

    def copy_of(kind, group, u, start, size):
        send_sem, recv_sem, peer = {'x': (x_send, x_recv, x_peer), 'd': (d_send, d_recv, d_peer), 'f': (f_send, f_recv, d_peer)}[kind]
        part = heads.at[group, pl.ds(start, size)]
        return pltpu.make_async_remote_copy(part, part, send_sem.at[u], recv_sem.at[u], device_id={'sp': peer}, device_id_type=MESH_ID)

    def publish(u, start, size):
        copy_of('x', s, u, start, size).start()
        copy_of('d', s, u, start, size).start()

    def forward(u):
        copy_of('x', x_peer, u, *units[u]).wait_recv()
        copy_of('f', x_peer, u, *units[u]).start()

    def multiply(t, k, width):
        part = jnp.dot(normed[:, rows_of(k)], wbuf[slot_of(t), :, pl.ds(0, width)], preferred_element_type=jnp.float32)

        @pl.when(k == 0)
        def _():
            acc[:, pl.ds(0, width)] = part

        @pl.when(k > 0)
        def _():
            acc[:, pl.ds(0, width)] += part

    def kv_step(t, carry):
        for cp in kv_copies(t):
            cp.wait()
        multiply(t, t, half)
        start_tile(t + SLOTS)
        return carry

    lax.fori_loop(0, n_k, kv_step, 0)
    heads[s, 0] = rope(acc[:, :HEAD], trig[0], trig[1])
    heads[s, 1] = acc[:, HEAD:2 * HEAD].astype(jnp.bfloat16).astype(jnp.float32)
    publish(0, *units[0])

    def wide_step(i, carry):
        t = i + t_wide
        k = lax.rem(i, n_k)
        chunk = lax.div(i, n_k)
        wide_copy(t).wait()
        multiply(t, k, WIDE)
        start_tile(t + SLOTS)

        @pl.when(k == n_k - 1)
        def _():
            first = 2 + 4 * chunk
            for h in range(4):
                heads[s, first + h] = rope(acc[:, h * HEAD:(h + 1) * HEAD], trig[0], trig[1])
            publish(chunk + 1, first, 4)

        for u in range(n_wide - 1):
            @pl.when(i == (u + 1) * n_k + 3)
            def _():
                forward(u)
        return carry

    lax.fori_loop(0, n_wide * n_k, wide_step, 0)

    def tail_step(i, carry):
        t = i + t_tail
        k = lax.rem(i, n_k)
        chunk = lax.div(i, n_k)
        tail_copy(t).wait()
        multiply(t, k, half)
        start_tile(t + SLOTS)

        @pl.when(k == n_k - 1)
        def _():
            first = 2 + 4 * n_wide + 2 * chunk
            for h in range(2):
                heads[s, first + h] = rope(acc[:, h * HEAD:(h + 1) * HEAD], trig[0], trig[1])
            publish(chunk + n_wide + 1, first, 2)

        for c in range(2):
            @pl.when(i == c * n_k + 4)
            def _():
                forward(n_wide - 1 + c)
        return carry

    lax.fori_loop(0, 2 * n_k, tail_step, 0)
    forward(n_wide + 1)
    forward(n_wide + 2)
    f_peer = lax.rem(d_peer + 2, 4)
    outs = [pltpu.make_async_copy(heads.at[g], out_hbm.at[g], out_sem.at[i]) for i, g in enumerate((s, x_peer, d_peer, f_peer))]
    outs[0].start()
    outs[1].start()
    for u, unit in enumerate(units):
        copy_of('d', d_peer, u, *unit).wait_recv()
    outs[2].start()
    for u, unit in enumerate(units):
        copy_of('f', f_peer, u, *unit).wait_recv()
    outs[3].start()
    for u, unit in enumerate(units):
        copy_of('x', s, u, *unit).wait_send()
        copy_of('d', s, u, *unit).wait_send()
        copy_of('f', x_peer, u, *unit).wait_send()
    for cp in outs:
        cp.wait()


def project(hidden, lengths, norm_gain, w_q, w_k, w_v, inv_freq):
    batch, dim = hidden.shape
    sp = 4
    n_head = w_q.shape[1] // sp // HEAD
    n_unit = n_head * HEAD // WIDE + 2
    freq = jnp.concatenate([inv_freq, inv_freq]).reshape(1, HEAD)
    vmem = pl.BlockSpec(memory_space=pltpu.VMEM)
    hbm = pl.BlockSpec(memory_space=pl.ANY)
    dma = pltpu.SemaphoreType.DMA
    return pl.pallas_call(
        qkv_kernel,
        out_shape=jax.ShapeDtypeStruct((sp, 2 + n_head, batch, HEAD), jnp.float32),
        in_specs=[pl.BlockSpec(memory_space=pltpu.SMEM), hbm, vmem, vmem, hbm, hbm, hbm],
        out_specs=hbm,
        scratch_shapes=[
            pltpu.VMEM((batch, dim), jnp.bfloat16),
            pltpu.VMEM((batch, dim), jnp.bfloat16),
            pltpu.VMEM((dim // HEAD, HEAD), jnp.float32),
            pltpu.VMEM((2, batch, HEAD), jnp.float32),
            pltpu.VMEM((SLOTS, KT, WIDE), jnp.bfloat16),
            pltpu.VMEM((batch, WIDE), jnp.float32),
            pltpu.VMEM((sp, 2 + n_head, batch, HEAD), jnp.float32),
            dma, dma((SLOTS,)), dma((SLOTS,)),
            dma((n_unit,)), dma((n_unit,)), dma((n_unit,)), dma((n_unit,)), dma((n_unit,)), dma((n_unit,)),
            dma((4,)),
        ],
        compiler_params=pltpu.CompilerParams(collective_id=0, has_side_effects=True, vmem_limit_bytes=60 * MIB),
        cost_estimate=pl.CostEstimate(flops=2 * batch * dim * (n_head + 2) * HEAD, bytes_accessed=2 * dim * (n_head + 2) * HEAD, transcendentals=0),
        name='qkv_exchange',
    )(lengths, hidden, norm_gain.reshape(dim // HEAD, HEAD), freq, w_q, w_k, w_v)


def attend_kernel(len_ref, k_hbm, v_hbm, qkv, k_out, v_out, o_ref, ml_ref,
                  kbuf, vbuf, slot_of, ml_rows, k_sem, v_sem, ko_sem, vo_sem):
    batch, rows, _ = k_hbm.shape
    n_kv = 4
    slots = rows // n_kv
    n_chunk = batch // SEQS
    n_unit = qkv.shape[0] // (n_kv * batch)
    group = n_unit - 2
    n_head = n_kv * group
    start = lax.axis_index('sp') * slots

    def in_copies(i):
        r = lax.rem(i, RING)
        seqs = pl.ds(i * SEQS, SEQS)
        return (pltpu.make_async_copy(k_hbm.at[seqs], kbuf.at[r], k_sem.at[r]),
                pltpu.make_async_copy(v_hbm.at[seqs], vbuf.at[r], v_sem.at[r]))

    def out_copies(i):
        r = lax.rem(i, RING)
        seqs = pl.ds(i * SEQS, SEQS)
        return (pltpu.make_async_copy(kbuf.at[r], k_out.at[seqs], ko_sem.at[r]),
                pltpu.make_async_copy(vbuf.at[r], v_out.at[seqs], vo_sem.at[r]))

    for i in range(AHEAD):
        for cp in in_copies(i):
            cp.start()

    row = lax.broadcasted_iota(jnp.int32, (n_head, rows), 0)
    col = lax.broadcasted_iota(jnp.int32, (n_head, rows), 1)
    slot_of[...] = jnp.where(lax.rem(col, n_kv) == lax.div(row, group), lax.div(col, n_kv), 2 ** 30)
    win_row = lax.broadcasted_iota(jnp.int32, (16, HEAD), 0)
    lane = lax.broadcasted_iota(jnp.int32, (n_head, HEAD), 1)

    def new_rows(offset, b):
        four = qkv[pl.ds(offset * batch + b, n_kv, stride=n_unit * batch), :]
        return jnp.concatenate([four] * 4, axis=0).astype(jnp.bfloat16)

    def chunk_step(i, carry):
        r = lax.rem(i, RING)

        @pl.when(i + AHEAD < n_chunk)
        def _():
            @pl.when(i + AHEAD >= RING)
            def _():
                for cp in out_copies(i + AHEAD - RING):
                    cp.wait()
            for cp in in_copies(i + AHEAD):
                cp.start()

        for cp in in_copies(i):
            cp.wait()
        for j in range(SEQS):
            b = i * SEQS + j
            pos = len_ref[b] - start
            held = jnp.clip(pos, 0, slots - 1)
            window = pl.ds(pl.multiple_of(lax.div(held, 4) * 16, 16), 16)
            pick = lax.div(win_row, n_kv) == jnp.where(held == pos, lax.rem(held, 4), -1)
            kbuf[r, j, window, :] = jnp.where(pick, new_rows(0, b), kbuf[r, j, window, :])
            vbuf[r, j, window, :] = jnp.where(pick, new_rows(1, b), vbuf[r, j, window, :])
        for cp in out_copies(i):
            cp.start()
        def scores_of(j):
            b = i * SEQS + j
            q = jnp.concatenate([qkv[pl.ds((g * n_unit + 2) * batch + b, group, stride=batch), :] for g in range(n_kv)], axis=0)
            return lax.dot_general(q.astype(jnp.bfloat16), kbuf[r, j], (((1,), (1,)), ((), ())), preferred_element_type=jnp.float32)

        def softmax_of(j, scores):
            valid = slot_of[...] <= len_ref[i * SEQS + j] - start
            scores = jnp.where(valid, scores, MASKED)
            top = jnp.max(scores, axis=1, keepdims=True)
            weights = jnp.where(valid, jnp.exp((scores - top) * SCALE), 0.0)
            return weights.astype(jnp.bfloat16), top, jnp.sum(weights, axis=1, keepdims=True)

        def finish(j, weights, top, total):
            b = i * SEQS + j
            o_ref[pl.ds(b, n_head, stride=batch), :] = jnp.dot(weights, vbuf[r, j], preferred_element_type=jnp.float32)
            ml_rows[pl.ds(b, n_head, stride=batch), :] = jnp.where(lane < n_head, top * SCALE, total)

        sc = [scores_of(j) for j in range(SEQS)]
        sm = [softmax_of(j, sc[j]) for j in range(SEQS)]
        for j in range(SEQS):
            finish(j, *sm[j])
        return carry

    lax.fori_loop(0, n_chunk, chunk_step, 0)
    out_lane = lax.broadcasted_iota(jnp.int32, (batch, HEAD), 1)

    def gather_step(h, acc):
        mine = lax.rem(out_lane, n_head) == h
        return jnp.where(mine, ml_rows[pl.ds(pl.multiple_of(h * batch, 8), batch), :], acc)

    ml_ref[...] = lax.fori_loop(0, n_head, gather_step, jnp.zeros((batch, HEAD), jnp.float32))

    def drain(i, carry):
        for cp in out_copies(i):
            cp.wait()
        return carry

    lax.fori_loop(n_chunk - RING, n_chunk, drain, 0)


def attend(qkv, lengths, k_cache, v_cache):
    batch, slots, n_kv, head = k_cache.shape
    rows = slots * n_kv
    n_head = n_kv * (qkv.shape[1] - 2)
    flat = (batch, rows, head)
    smem = pl.BlockSpec(memory_space=pltpu.SMEM)
    vmem = pl.BlockSpec(memory_space=pltpu.VMEM)
    hbm = pl.BlockSpec(memory_space=pl.ANY)
    dma = pltpu.SemaphoreType.DMA((RING,))
    k_new, v_new, out, ml = pl.pallas_call(
        attend_kernel,
        out_shape=(jax.ShapeDtypeStruct(flat, jnp.bfloat16), jax.ShapeDtypeStruct(flat, jnp.bfloat16),
                   jax.ShapeDtypeStruct((n_head * batch, head), jnp.float32), jax.ShapeDtypeStruct((batch, head), jnp.float32)),
        in_specs=[smem, hbm, hbm, vmem],
        out_specs=(hbm, hbm, vmem, vmem),
        scratch_shapes=[
            pltpu.VMEM((RING, SEQS, rows, head), jnp.bfloat16),
            pltpu.VMEM((RING, SEQS, rows, head), jnp.bfloat16),
            pltpu.VMEM((n_head, rows), jnp.int32),
            pltpu.VMEM((n_head * batch, head), jnp.float32),
            dma, dma, dma, dma,
        ],
        compiler_params=pltpu.CompilerParams(vmem_limit_bytes=50 * MIB),
        cost_estimate=pl.CostEstimate(flops=4 * batch * n_head * rows * head, bytes_accessed=8 * batch * rows * head, transcendentals=0),
        name='attend_local',
    )(lengths, k_cache.reshape(flat), v_cache.reshape(flat), qkv.reshape(-1, head))
    return k_new.reshape(k_cache.shape), v_new.reshape(v_cache.shape), out, ml


def combine_kernel(o_hbm, ml_ref, hid_hbm, wo, y_hbm,
                   own, other, ml_all, gates, mine, x_out, x_in, d_out, d_in, obf, hid, wbuf,
                   part, part_in, fin, fin_x, fin_d, fin_f, ybf,
                   own_sem, hid_sem, w_sem, y_sem, ml_send, ml_recv, o_send, o_recv, x_send, x_recv, d_send, d_recv,
                   p_send, p_recv, fx_send, fx_recv, fd_send, fd_recv, ff_send, ff_recv):
    n_head, batch, _ = o_hbm.shape
    rows = batch // 2
    half = n_head // 2
    n_piece = half // PIECE
    n_k = wo.shape[0] // OUT_K
    cols = wo.shape[1] // 2
    n_col = cols // OUT_W
    n_tile = n_col * n_k
    tp = lax.axis_index('tp')
    s = lax.axis_index('sp')
    x = lax.div(s, 2)
    c = lax.rem(s, 2)
    x_peer = lax.rem(s + 2, 4)
    d_peer = s + 1 - 2 * c
    diag = 3 - s
    my_rows = pl.ds(pl.multiple_of(x * rows, 16), rows)
    peer_rows = pl.ds(pl.multiple_of((1 - x) * rows, 16), rows)

    def remote(src, dst, send_sem, recv_sem, peer):
        device = {'sp': peer} if peer is not None else {'tp': 1 - tp}
        return pltpu.make_async_remote_copy(src, dst, send_sem, recv_sem, device_id=device, device_id_type=MESH_ID)

    def w_copy(t):
        lanes = pl.ds(pl.multiple_of(c * cols + lax.div(t, n_k) * OUT_W, OUT_W), OUT_W)
        depth = pl.ds(pl.multiple_of(lax.rem(t, n_k) * OUT_K, OUT_K), OUT_K)
        slot = lax.rem(t, OUT_SLOTS)
        return pltpu.make_async_copy(wo.at[depth, lanes], wbuf.at[slot], w_sem.at[slot])

    own_copy = pltpu.make_async_copy(o_hbm.at[pl.ds(c * half, half)], own, own_sem)
    own_copy.start()
    hid_copy = pltpu.make_async_copy(hid_hbm.at[my_rows, pl.ds(pl.multiple_of(c * cols, cols), cols)], hid, hid_sem)
    hid_copy.start()
    for t in range(OUT_SLOTS):
        w_copy(t).start(priority=1)

    barrier = pltpu.get_barrier_semaphore()
    for device in ({'sp': x_peer}, {'sp': d_peer}, {'sp': diag}, {'tp': 1 - tp}):
        pl.semaphore_signal(barrier, inc=1, device_id=device, device_id_type=MESH_ID)
    pl.semaphore_wait(barrier, 4)

    ml_copies = [remote(ml_ref, ml_all.at[i], ml_send.at[i], ml_recv.at[i], peer) for i, peer in enumerate((x_peer, d_peer, diag))]
    for cp in ml_copies:
        cp.start()

    def o_copy(p):
        return remote(o_hbm.at[pl.ds((1 - c) * half + p * PIECE, PIECE)], other.at[pl.ds(p * PIECE, PIECE)], o_send.at[p], o_recv.at[p], d_peer)

    for p in range(n_piece):
        o_copy(p).start()

    for cp in ml_copies:
        cp.wait()
    stats = [ml_ref[...], ml_all[1], ml_all[0], ml_all[2]]
    top = functools.reduce(jnp.maximum, stats)
    factors = [jnp.exp(m - top) for m in stats]
    total = functools.reduce(jnp.add, [f * pltpu.roll(m, n_head, 1) for f, m in zip(factors, stats)])
    for i in range(2):
        gate = factors[i] / total
        gates[i] = jnp.where(c == 0, gate, pltpu.roll(gate, HEAD - half, 1))
    own_copy.wait()

    def x_copy(p):
        part_of = pl.ds(p * PIECE, PIECE)
        return remote(x_out.at[part_of], x_in.at[part_of], x_send.at[p], x_recv.at[p], x_peer)

    def weigh(p, which):
        mine_gate = gates[0, which, :]
        other_gate = gates[1, which, :]
        out = []
        for h in range(PIECE):
            i = p * PIECE + h
            out.append(mine_gate[:, h:h + 1] * own[i, which, :] + other_gate[:, h:h + 1] * other[i, which, :])
        return out

    def mix_step(p, carry):
        o_copy(p).wait_recv()
        for h, val in enumerate(weigh(p, peer_rows)):
            x_out[p * PIECE + h] = val
        x_copy(p).start()
        for h, val in enumerate(weigh(p, my_rows)):
            mine[p * PIECE + h] = val
        gates[0] = pltpu.roll(gates[0], HEAD - PIECE, 1)
        gates[1] = pltpu.roll(gates[1], HEAD - PIECE, 1)
        return carry

    lax.fori_loop(0, n_piece, mix_step, 0)

    def d_copy(p):
        part_of = pl.ds(p * PIECE, PIECE)
        return remote(d_out.at[part_of], d_in.at[part_of], d_send.at[p], d_recv.at[p], d_peer)

    def head_lanes(h):
        return pl.ds(pl.multiple_of(h * HEAD, HEAD), HEAD)

    def merge_step(p, carry):
        x_copy(p).wait_recv()
        for h in range(PIECE):
            i = p * PIECE + h
            val = (mine[i] + x_in[i]).astype(jnp.bfloat16)
            obf[:, head_lanes(c * half + i)] = val
            d_out[i] = val.astype(jnp.float32)
        d_copy(p).start()
        return carry

    lax.fori_loop(0, n_piece, merge_step, 0)

    def spread_step(p, carry):
        d_copy(p).wait_recv()
        for h in range(PIECE):
            i = p * PIECE + h
            obf[:, head_lanes((1 - c) * half + i)] = d_in[i].astype(jnp.bfloat16)
        return carry

    lax.fori_loop(0, n_piece, spread_step, 0)
    hid_copy.wait()

    def p_copy(j):
        return remote(part.at[j], part_in.at[j], p_send.at[j], p_recv.at[j], None)

    def fx_copy(j):
        return remote(fin.at[j], fin_x.at[j], fx_send.at[j], fx_recv.at[j], x_peer)

    def fd_copy(j):
        return remote(fin.at[j], fin_d.at[j], fd_send.at[j], fd_recv.at[j], d_peer)

    def ff_copy(j):
        return remote(fin_x.at[j], fin_f.at[j], ff_send.at[j], ff_recv.at[j], d_peer)

    def lanes_of(j, core):
        return pl.ds(pl.multiple_of(core * cols + j * OUT_W, OUT_W), OUT_W)

    def y_copies(j):
        return [pltpu.make_async_copy(ybf.at[:, lanes_of(j, core)], y_hbm.at[:, lanes_of(j, core)], y_sem.at[core, j]) for core in range(2)]

    def finish(j):
        p_copy(j).wait_recv()
        lane = pl.ds(pl.multiple_of(j * OUT_W, OUT_W), OUT_W)
        val = (hid[:, lane].astype(jnp.float32) + (part[j] + part_in[j])).astype(jnp.bfloat16)
        ybf[my_rows, lanes_of(j, c)] = val
        fin[j] = val.astype(jnp.float32)
        fx_copy(j).start()
        fd_copy(j).start()

    def pass_on(j):
        fx_copy(j).wait_recv()
        ff_copy(j).start()
        ybf[peer_rows, lanes_of(j, c)] = fin_x[j].astype(jnp.bfloat16)
        fd_copy(j).wait_recv()
        ybf[my_rows, lanes_of(j, 1 - c)] = fin_d[j].astype(jnp.bfloat16)

    def deliver(j):
        ff_copy(j).wait_recv()
        ybf[peer_rows, lanes_of(j, 1 - c)] = fin_f[j].astype(jnp.bfloat16)
        for cp in y_copies(j):
            cp.start()

    lags = (2, 4, 5)

    def col_step(j, carry):
        @pl.when(j < n_col)
        def _():
            acc = None
            for k in range(n_k):
                t = j * n_k + k
                w_copy(t).wait()
                term = jnp.dot(obf[:, k * OUT_K:(k + 1) * OUT_K], wbuf[lax.rem(t, OUT_SLOTS)], preferred_element_type=jnp.float32)
                acc = term if acc is None else acc + term

                @pl.when(t + OUT_SLOTS < n_tile)
                def _():
                    w_copy(t + OUT_SLOTS).start(priority=1)
            part[j] = acc
            p_copy(j).start()

        for lag, stage in zip(lags, (finish, pass_on, deliver)):
            @pl.when((j >= lag) & (j - lag < n_col))
            def _():
                stage(j - lag)
        return carry

    lax.fori_loop(0, n_col + lags[-1], col_step, 0)

    for p in range(n_piece):
        o_copy(p).wait_send()
        x_copy(p).wait_send()
        d_copy(p).wait_send()

    def drain(j, carry):
        p_copy(j).wait_send()
        fx_copy(j).wait_send()
        fd_copy(j).wait_send()
        ff_copy(j).wait_send()
        for cp in y_copies(j):
            cp.wait()
        return carry

    lax.fori_loop(0, n_col, drain, 0)


def combine(out, ml, hidden, w_o):
    batch, dim = hidden.shape
    n_head = out.shape[0] // batch
    rows = batch // 2
    half = n_head // 2
    n_piece = half // PIECE
    n_col = dim // 2 // OUT_W
    vmem = pl.BlockSpec(memory_space=pltpu.VMEM)
    hbm = pl.BlockSpec(memory_space=pl.ANY)
    dma = pltpu.SemaphoreType.DMA
    f32 = jnp.float32
    quad = pltpu.VMEM((half, rows, HEAD), f32)
    tiles = pltpu.VMEM((n_col, rows, OUT_W), f32)
    return pl.pallas_call(
        combine_kernel,
        out_shape=jax.ShapeDtypeStruct((batch, dim), jnp.bfloat16),
        in_specs=[hbm, vmem, hbm, hbm],
        out_specs=hbm,
        scratch_shapes=[
            pltpu.VMEM((half, batch, HEAD), f32), pltpu.VMEM((half, batch, HEAD), f32),
            pltpu.VMEM((3, batch, HEAD), f32), pltpu.VMEM((2, batch, HEAD), f32),
            quad, quad, quad, quad, quad,
            pltpu.VMEM((rows, n_head * HEAD), jnp.bfloat16), pltpu.VMEM((rows, dim // 2), jnp.bfloat16),
            pltpu.VMEM((OUT_SLOTS, OUT_K, OUT_W), jnp.bfloat16),
            tiles, tiles, tiles, tiles, tiles, tiles,
            pltpu.VMEM((batch, dim), jnp.bfloat16),
            dma, dma, dma((OUT_SLOTS,)), dma((2, n_col)), dma((3,)), dma((3,)),
            dma((n_piece,)), dma((n_piece,)), dma((n_piece,)), dma((n_piece,)), dma((n_piece,)), dma((n_piece,)),
            dma((n_col,)), dma((n_col,)), dma((n_col,)), dma((n_col,)), dma((n_col,)), dma((n_col,)), dma((n_col,)), dma((n_col,)),
        ],
        compiler_params=pltpu.CompilerParams(collective_id=1, has_side_effects=True, vmem_limit_bytes=63 * MIB),
        cost_estimate=pl.CostEstimate(flops=batch * dim * n_head * HEAD, bytes_accessed=dim * n_head * HEAD, transcendentals=0),
        name='combine_project',
    )(out.reshape(n_head, batch, HEAD), ml, hidden, w_o)


def device_step(hidden, lengths, k_cache, v_cache, norm_gain, w_q, w_k, w_v, w_o, inv_freq):
    qkv = project(hidden, lengths, norm_gain, w_q, w_k, w_v, inv_freq)
    k_new, v_new, out, ml = attend(qkv, lengths, k_cache, v_cache)
    return combine(out, ml, hidden, w_o), k_new, v_new


def solution(mesh):
    cache_spec = P('dp', 'sp', 'tp', None)
    in_specs = (P('dp', None), P('dp'), cache_spec, cache_spec, P(None), P(None, 'tp'), P(None, 'tp'), P(None, 'tp'), P('tp', None), P(None))
    out_specs = (P('dp', None), cache_spec, cache_spec)
    return jax.shard_map(device_step, mesh=mesh, in_specs=in_specs, out_specs=out_specs, check_vma=False)
```

time: 535 us -> 137 us (0.26)
  matrix products: 214 us -> 0 us
  waiting for transfers between devices: 198 us -> 0 us
  Pallas kernels: 0 us -> 129 us
  local copies, waits for them, and re-layouts: 48.7 us -> 6.03 us
  blocking collectives: 33.8 us -> 0 us
  other arithmetic: 25.2 us -> 1.31 us
  between operations: 14.2 us -> 0.67 us
    dot_general x6 -> x0, matrix products: 214 us -> none  [the longest x1 85.7 us: project_new_token(): jnp.dot(normed, w_q, preferred_element_type=jnp.float32)]
    psum x1 -> x0, waiting for transfers between devices: 148 us -> none  [device_step(): lax.psum(jnp.dot(attn_out, w_o, preferred_element_type=jnp.float32), 'tp')]
    pallas_call x0 -> x3, Pallas kernels: none -> 129 us  [the longest x1 71.3 us: combine(): pl.pallas_call(combine_kernel, out_shape=jax.ShapeDtypeStruct((batch, dim...]
    all_gather x1 -> x0, waiting for transfers between devices: 50.1 us -> none  [device_step(): all_out = lax.all_gather(part_out, 'sp')]
    all_gather x2 -> x0, blocking collectives: 33.8 us -> none  [the longest x1 19.9 us: device_step(): all_sum = lax.all_gather(part_sum, 'sp')]
    scatter x2 -> x0, local copies, waits for them, and re-layouts: 27.4 us -> none  [the longest x1 13.8 us: write_and_attend(): k_upd = k_cache.at[row_ids, write_pos].set(k_rot, mode='drop')]
    unnamed x15 -> x7, local copies, waits for them, and re-layouts: 20.3 us -> 6.03 us
    reduce_sum x4 -> x0, other arithmetic: 13.2 us -> none  [the longest x1 7.87 us: device_step(): weighted = jnp.sum(factor[..., None] * all_out, axis=0)]
  transfers between devices with their start and end apart: 2 -> 0, of which waited for: 2 -> 0; matrix products, arithmetic and copies ran while one was open for 1% -> 0% of each run, Pallas kernels for 0% -> 0%
where the time goes in v1:
time: 137 us
  Pallas kernels  129 us (94%)
  local copies, waits for them, and re-layouts  6.03 us (4%)
    pallas_call x1, Pallas kernels, combine(): pl.pallas_call(combine_kernel, out_shape=jax.ShapeDtypeStruct((batch, dim...  71.3 us
    pallas_call x1, Pallas kernels, project(): pl.pallas_call(qkv_kernel, out_shape=jax.ShapeDtypeStruct((sp, 2 + n_head...  36.9 us
    pallas_call x1, Pallas kernels, attend(): pl.pallas_call(attend_kernel, out_shape=(jax.ShapeDtypeStruct(flat, jnp.b...  20.5 us
    unnamed x7, local copies, waits for them, and re-layouts  6.03 us

profile of v1, /device:TPU:0, one launch (start us, length us, event | category | flops | bytes accessed | tf_op | source)
XLA Modules:
  0.0 136.7 jit_solution(366548810209316134)
XLA Ops:
  0.6 1.3 maximum_bitcast_fusion.freq_ref
  1.9 0.0 copy-start.2
  1.9 36.9 %qkv_exchange.1 = f32[4,18,96,128]{3,2,1,0:T(8,128)} custom-call(s32[96]{0:T(128)} %len_ref.3, bf16[96,16384]{1,0:T(8,128)(2,1)} %hid_hbm.3, bf16[128,128]{1,0:T(8,128)(2,1)} %bitcast.13, f32[1,128]{1,0:T(1,128)} %maximum_bitcast_fusion.freq_ref, bf16[16384,8192]{1,0:T(8,128)(2,1)} %wq.1, bf16[16384,512]{1,0:T(8,128)(2,1)} %wk.1, bf16[16384,512]{1,0:T(8,128)(2,1)} %wv.1), custom_call_target="tpu_custom_call" | custom-call | flops 7247757312 | bytes 75497472 | tf_op jit(solution)/shard_map/qkv_exchange/pallas_call | solution.py:244
  38.8 0.0 copy-done.2
  38.8 20.5 %attend_local.1 = (bf16[96,512,128]{2,1,0:T(8,128)(2,1)}, bf16[96,512,128]{2,1,0:T(8,128)(2,1)}, f32[6144,128]{1,0:T(8,128)S(1)}, f32[96,128]{1,0:T(8,128)S(1)}) custom-call(s32[96]{0:T(128)S(1)} %copy-done.2, bf16[96,512,128]{2,1,0:T(8,128)(2,1)} %bitcast.11, bf16[96,512,128]{2,1,0:T(8,128)(2,1)} %bitcast.12, f32[6912,128]{1,0:T(8,128)} %bitcast.10), custom_call_target="tpu_custom_call" | custom-call | flops 1610612736 | bytes 50331648 | tf_op jit(solution)/shard_map/attend_local/pallas_call | solution.py:377
  59.3 0.0 copy-start
  59.3 1.7 %copy-done = f32[6144,128]{1,0:T(8,128)} copy-done((f32[6144,128]{1,0:T(8,128)}, f32[6144,128]{1,0:T(8,128)S(1)}, u32[]{:S(2)}) %copy-start) | copy-done | bytes 3145752
  61.0 0.0 copy-start.1
  61.0 0.6 copy-done.1
  61.6 71.3 %combine_project.1 = bf16[96,16384]{1,0:T(8,128)(2,1)} custom-call(f32[64,96,128]{2,1,0:T(8,128)} %bitcast.9, f32[96,128]{1,0:T(8,128)} %copy-done.1, bf16[96,16384]{1,0:T(8,128)(2,1)} %hid_hbm.3, bf16[8192,16384]{1,0:T(8,128)(2,1)} %wo.1), custom_call_target="tpu_custom_call" | custom-call | flops 12884901888 | bytes 134217728 | tf_op jit(solution)/shard_map/combine_project/pallas_call | solution.py:614
  132.9 3.8 %copy.14 = bf16[96,16384]{1,0:T(8,128)(2,1)} copy(bf16[96,16384]{1,0:T(8,128)(2,1)} %combine_project.1) | data formatting | bytes 6291456
Async XLA Ops:
  1.9 36.9 %copy-start.2 = (s32[96]{0:T(128)S(1)}, s32[96]{0:T(128)}, u32[]{:S(2)}) copy-start(s32[96]{0:T(128)} %len_ref.3) | copy-start | bytes 1156
  59.3 1.7 %copy-start = (f32[6144,128]{1,0:T(8,128)}, f32[6144,128]{1,0:T(8,128)S(1)}, u32[]{:S(2)}) copy-start(f32[6144,128]{1,0:T(8,128)S(1)} %get-tuple-element.7) | copy-start | bytes 9437188
  61.0 0.6 copy-start.1

commit v2 on v1

--- a/solution.py
+++ b/solution.py
@@ -11,7 +11,7 @@
 HEAD = 128
 KT = 2048
 WIDE = 512
-SLOTS = 12
+SLOTS = 16
 MIB = 2 ** 20
 MESH_ID = pl.DeviceIdType.MESH
 SEQS = 8
@@ -19,9 +19,9 @@
 AHEAD = 4
 MASKED = -3e38
 SCALE = HEAD ** -0.5
-OUT_K = 4096
-OUT_W = 512
-OUT_SLOTS = 9
+OUT_K = 8192
+OUT_W = 256
+OUT_SLOTS = 6
 PIECE = 8
 
 
@@ -91,9 +91,8 @@
     barrier = pltpu.get_barrier_semaphore()
     for peer in (x_peer, d_peer):
         pl.semaphore_signal(barrier, inc=1, device_id={'sp': peer}, device_id_type=MESH_ID)
-    pl.semaphore_wait(barrier, 2)
-
-    freq = freq_ref[...]
+
+    freq = jnp.concatenate([freq_ref[...], freq_ref[...]], axis=1)
 
     def angle_step(b, carry):
         trig[0, pl.ds(b, 1), :] = len_ref[b].astype(jnp.float32) * freq
@@ -163,6 +162,7 @@
         return carry
 
     lax.fori_loop(0, n_k, kv_step, 0)
+    pl.semaphore_wait(barrier, 2)
     heads[s, 0] = rope(acc[:, :HEAD], trig[0], trig[1])
     heads[s, 1] = acc[:, HEAD:2 * HEAD].astype(jnp.bfloat16).astype(jnp.float32)
     publish(0, *units[0])
@@ -237,7 +237,6 @@
     sp = 4
     n_head = w_q.shape[1] // sp // HEAD
     n_unit = n_head * HEAD // WIDE + 2
-    freq = jnp.concatenate([inv_freq, inv_freq]).reshape(1, HEAD)
     vmem = pl.BlockSpec(memory_space=pltpu.VMEM)
     hbm = pl.BlockSpec(memory_space=pl.ANY)
     dma = pltpu.SemaphoreType.DMA
@@ -261,11 +260,11 @@
         compiler_params=pltpu.CompilerParams(collective_id=0, has_side_effects=True, vmem_limit_bytes=60 * MIB),
         cost_estimate=pl.CostEstimate(flops=2 * batch * dim * (n_head + 2) * HEAD, bytes_accessed=2 * dim * (n_head + 2) * HEAD, transcendentals=0),
         name='qkv_exchange',
-    )(lengths, hidden, norm_gain.reshape(dim // HEAD, HEAD), freq, w_q, w_k, w_v)
-
-
-def attend_kernel(len_ref, k_hbm, v_hbm, qkv, k_out, v_out, o_ref, ml_ref,
-                  kbuf, vbuf, slot_of, ml_rows, k_sem, v_sem, ko_sem, vo_sem):
+    )(lengths, hidden, norm_gain.reshape(dim // HEAD, HEAD), inv_freq.reshape(1, HEAD // 2), w_q, w_k, w_v)
+
+
+def attend_kernel(len_ref, k_hbm, v_hbm, qkv_hbm, k_out, v_out, o_ref, ml_ref,
+                  qkv, qkv_sem, kbuf, vbuf, slot_of, ml_rows, k_sem, v_sem, ko_sem, vo_sem):
     batch, rows, _ = k_hbm.shape
     n_kv = 4
     slots = rows // n_kv
@@ -287,6 +286,8 @@
         return (pltpu.make_async_copy(kbuf.at[r], k_out.at[seqs], ko_sem.at[r]),
                 pltpu.make_async_copy(vbuf.at[r], v_out.at[seqs], vo_sem.at[r]))
 
+    qkv_copy = pltpu.make_async_copy(qkv_hbm, qkv, qkv_sem)
+    qkv_copy.start()
     for i in range(AHEAD):
         for cp in in_copies(i):
             cp.start()
@@ -296,6 +297,8 @@
     slot_of[...] = jnp.where(lax.rem(col, n_kv) == lax.div(row, group), lax.div(col, n_kv), 2 ** 30)
     win_row = lax.broadcasted_iota(jnp.int32, (16, HEAD), 0)
     lane = lax.broadcasted_iota(jnp.int32, (n_head, HEAD), 1)
+
+    qkv_copy.wait()
 
     def new_rows(offset, b):
         four = qkv[pl.ds(offset * batch + b, n_kv, stride=n_unit * batch), :]
@@ -378,9 +381,10 @@
         attend_kernel,
         out_shape=(jax.ShapeDtypeStruct(flat, jnp.bfloat16), jax.ShapeDtypeStruct(flat, jnp.bfloat16),
                    jax.ShapeDtypeStruct((n_head * batch, head), jnp.float32), jax.ShapeDtypeStruct((batch, head), jnp.float32)),
-        in_specs=[smem, hbm, hbm, vmem],
+        in_specs=[smem, hbm, hbm, hbm],
         out_specs=(hbm, hbm, vmem, vmem),
         scratch_shapes=[
+            pltpu.VMEM((qkv.shape[0] * qkv.shape[1] * batch, head), jnp.float32), pltpu.SemaphoreType.DMA,
             pltpu.VMEM((RING, SEQS, rows, head), jnp.bfloat16),
             pltpu.VMEM((RING, SEQS, rows, head), jnp.bfloat16),
             pltpu.VMEM((n_head, rows), jnp.int32),
@@ -394,12 +398,12 @@
     return k_new.reshape(k_cache.shape), v_new.reshape(v_cache.shape), out, ml
 
 
-def combine_kernel(o_hbm, ml_ref, hid_hbm, wo, y_hbm,
-                   own, other, ml_all, gates, mine, x_out, x_in, d_out, d_in, obf, hid, wbuf,
-                   part, part_in, fin, fin_x, fin_d, fin_f, ybf,
-                   own_sem, hid_sem, w_sem, y_sem, ml_send, ml_recv, o_send, o_recv, x_send, x_recv, d_send, d_recv,
+def combine_kernel(own, ml_ref, hid_hbm, wo, ybf,
+                   other, ml_in, ml_chip, gates, mine, x_out, x_in, d_out, d_in, obf, hid, wbuf,
+                   part, part_in, fin, fin_x, fin_d, fin_f,
+                   hid_sem, w_sem, ml_send, ml_recv, o_send, o_recv, x_send, x_recv, d_send, d_recv,
                    p_send, p_recv, fx_send, fx_recv, fd_send, fd_recv, ff_send, ff_recv):
-    n_head, batch, _ = o_hbm.shape
+    n_head, batch, _ = own.shape
     rows = batch // 2
     half = n_head // 2
     n_piece = half // PIECE
@@ -413,7 +417,6 @@
     c = lax.rem(s, 2)
     x_peer = lax.rem(s + 2, 4)
     d_peer = s + 1 - 2 * c
-    diag = 3 - s
     my_rows = pl.ds(pl.multiple_of(x * rows, 16), rows)
     peer_rows = pl.ds(pl.multiple_of((1 - x) * rows, 16), rows)
 
@@ -427,38 +430,42 @@
         slot = lax.rem(t, OUT_SLOTS)
         return pltpu.make_async_copy(wo.at[depth, lanes], wbuf.at[slot], w_sem.at[slot])
 
-    own_copy = pltpu.make_async_copy(o_hbm.at[pl.ds(c * half, half)], own, own_sem)
-    own_copy.start()
     hid_copy = pltpu.make_async_copy(hid_hbm.at[my_rows, pl.ds(pl.multiple_of(c * cols, cols), cols)], hid, hid_sem)
     hid_copy.start()
     for t in range(OUT_SLOTS):
         w_copy(t).start(priority=1)
 
     barrier = pltpu.get_barrier_semaphore()
-    for device in ({'sp': x_peer}, {'sp': d_peer}, {'sp': diag}, {'tp': 1 - tp}):
+    for device in ({'sp': x_peer}, {'sp': d_peer}, {'tp': 1 - tp}):
         pl.semaphore_signal(barrier, inc=1, device_id=device, device_id_type=MESH_ID)
-    pl.semaphore_wait(barrier, 4)
-
-    ml_copies = [remote(ml_ref, ml_all.at[i], ml_send.at[i], ml_recv.at[i], peer) for i, peer in enumerate((x_peer, d_peer, diag))]
-    for cp in ml_copies:
-        cp.start()
+    pl.semaphore_wait(barrier, 3)
+
+    ml_partner = remote(ml_ref, ml_in.at[0], ml_send.at[0], ml_recv.at[0], d_peer)
+    ml_partner.start()
 
     def o_copy(p):
-        return remote(o_hbm.at[pl.ds((1 - c) * half + p * PIECE, PIECE)], other.at[pl.ds(p * PIECE, PIECE)], o_send.at[p], o_recv.at[p], d_peer)
+        return remote(own.at[pl.ds((1 - c) * half + p * PIECE, PIECE)], other.at[pl.ds(p * PIECE, PIECE)], o_send.at[p], o_recv.at[p], d_peer)
 
     for p in range(n_piece):
         o_copy(p).start()
 
-    for cp in ml_copies:
-        cp.wait()
-    stats = [ml_ref[...], ml_all[1], ml_all[0], ml_all[2]]
-    top = functools.reduce(jnp.maximum, stats)
-    factors = [jnp.exp(m - top) for m in stats]
-    total = functools.reduce(jnp.add, [f * pltpu.roll(m, n_head, 1) for f, m in zip(factors, stats)])
+    lane = lax.broadcasted_iota(jnp.int32, (batch, HEAD), 1)
+
+    def merge_stats(first, second):
+        top = jnp.maximum(first, second)
+        factors = [jnp.exp(jnp.where(lane < n_head, m - top, 0.0)) for m in (first, second)]
+        total = functools.reduce(jnp.add, [f * pltpu.roll(m, n_head, 1) for f, m in zip(factors, (first, second))])
+        return top, factors, total
+
+    def local_heads(per_head):
+        return jnp.where(c == 0, per_head, pltpu.roll(per_head, HEAD - half, 1))
+
+    ml_partner.wait()
+    top, factors, total = merge_stats(ml_ref[...], ml_in[0])
+    ml_chip[...] = jnp.where(lane < n_head, top, pltpu.roll(total, n_head, 1))
     for i in range(2):
-        gate = factors[i] / total
-        gates[i] = jnp.where(c == 0, gate, pltpu.roll(gate, HEAD - half, 1))
-    own_copy.wait()
+        gates[i] = local_heads(factors[i])
+    ml_x = remote(ml_chip, ml_in.at[1], ml_send.at[1], ml_recv.at[1], x_peer)
 
     def x_copy(p):
         part_of = pl.ds(p * PIECE, PIECE)
@@ -470,7 +477,7 @@
         out = []
         for h in range(PIECE):
             i = p * PIECE + h
-            out.append(mine_gate[:, h:h + 1] * own[i, which, :] + other_gate[:, h:h + 1] * other[i, which, :])
+            out.append(mine_gate[:, h:h + 1] * own[c * half + i, which, :] + other_gate[:, h:h + 1] * other[i, which, :])
         return out
 
     def mix_step(p, carry):
@@ -478,6 +485,11 @@
         for h, val in enumerate(weigh(p, peer_rows)):
             x_out[p * PIECE + h] = val
         x_copy(p).start()
+
+        @pl.when(p == 0)
+        def _():
+            ml_x.start()
+
         for h, val in enumerate(weigh(p, my_rows)):
             mine[p * PIECE + h] = val
         gates[0] = pltpu.roll(gates[0], HEAD - PIECE, 1)
@@ -485,6 +497,10 @@
         return carry
 
     lax.fori_loop(0, n_piece, mix_step, 0)
+    ml_x.wait()
+    top, factors, total = merge_stats(ml_chip[...], ml_in[1])
+    for i in range(2):
+        gates[i] = local_heads(factors[i] / total)
 
     def d_copy(p):
         part_of = pl.ds(p * PIECE, PIECE)
@@ -495,12 +511,16 @@
 
     def merge_step(p, carry):
         x_copy(p).wait_recv()
+        mine_gate = gates[0, my_rows, :]
+        in_gate = gates[1, my_rows, :]
         for h in range(PIECE):
             i = p * PIECE + h
-            val = (mine[i] + x_in[i]).astype(jnp.bfloat16)
+            val = (mine_gate[:, h:h + 1] * mine[i] + in_gate[:, h:h + 1] * x_in[i]).astype(jnp.bfloat16)
             obf[:, head_lanes(c * half + i)] = val
             d_out[i] = val.astype(jnp.float32)
         d_copy(p).start()
+        gates[0] = pltpu.roll(gates[0], HEAD - PIECE, 1)
+        gates[1] = pltpu.roll(gates[1], HEAD - PIECE, 1)
         return carry
 
     lax.fori_loop(0, n_piece, merge_step, 0)
@@ -529,9 +549,6 @@
 
     def lanes_of(j, core):
         return pl.ds(pl.multiple_of(core * cols + j * OUT_W, OUT_W), OUT_W)
-
-    def y_copies(j):
-        return [pltpu.make_async_copy(ybf.at[:, lanes_of(j, core)], y_hbm.at[:, lanes_of(j, core)], y_sem.at[core, j]) for core in range(2)]
 
     def finish(j):
         p_copy(j).wait_recv()
@@ -552,10 +569,8 @@
     def deliver(j):
         ff_copy(j).wait_recv()
         ybf[peer_rows, lanes_of(j, 1 - c)] = fin_f[j].astype(jnp.bfloat16)
-        for cp in y_copies(j):
-            cp.start()
-
-    lags = (2, 4, 5)
+
+    lags = (4, 8, 10)
 
     def col_step(j, carry):
         @pl.when(j < n_col)
@@ -591,8 +606,6 @@
         fx_copy(j).wait_send()
         fd_copy(j).wait_send()
         ff_copy(j).wait_send()
-        for cp in y_copies(j):
-            cp.wait()
         return carry
 
     lax.fori_loop(0, n_col, drain, 0)
@@ -614,21 +627,20 @@
     return pl.pallas_call(
         combine_kernel,
         out_shape=jax.ShapeDtypeStruct((batch, dim), jnp.bfloat16),
-        in_specs=[hbm, vmem, hbm, hbm],
-        out_specs=hbm,
+        in_specs=[vmem, vmem, hbm, hbm],
+        out_specs=vmem,
         scratch_shapes=[
-            pltpu.VMEM((half, batch, HEAD), f32), pltpu.VMEM((half, batch, HEAD), f32),
-            pltpu.VMEM((3, batch, HEAD), f32), pltpu.VMEM((2, batch, HEAD), f32),
+            pltpu.VMEM((half, batch, HEAD), f32),
+            pltpu.VMEM((2, batch, HEAD), f32), pltpu.VMEM((batch, HEAD), f32), pltpu.VMEM((2, batch, HEAD), f32),
             quad, quad, quad, quad, quad,
             pltpu.VMEM((rows, n_head * HEAD), jnp.bfloat16), pltpu.VMEM((rows, dim // 2), jnp.bfloat16),
             pltpu.VMEM((OUT_SLOTS, OUT_K, OUT_W), jnp.bfloat16),
             tiles, tiles, tiles, tiles, tiles, tiles,
-            pltpu.VMEM((batch, dim), jnp.bfloat16),
-            dma, dma, dma((OUT_SLOTS,)), dma((2, n_col)), dma((3,)), dma((3,)),
+            dma, dma((OUT_SLOTS,)), dma((2,)), dma((2,)),
             dma((n_piece,)), dma((n_piece,)), dma((n_piece,)), dma((n_piece,)), dma((n_piece,)), dma((n_piece,)),
             dma((n_col,)), dma((n_col,)), dma((n_col,)), dma((n_col,)), dma((n_col,)), dma((n_col,)), dma((n_col,)), dma((n_col,)),
         ],
-        compiler_params=pltpu.CompilerParams(collective_id=1, has_side_effects=True, vmem_limit_bytes=63 * MIB),
+        compiler_params=pltpu.CompilerParams(collective_id=1, has_side_effects=True, vmem_limit_bytes=46 * MIB),
         cost_estimate=pl.CostEstimate(flops=batch * dim * n_head * HEAD, bytes_accessed=dim * n_head * HEAD, transcendentals=0),
         name='combine_project',
     )(out.reshape(n_head, batch, HEAD), ml, hidden, w_o)

time: 137 us -> 131 us (0.956)
  local copies, waits for them, and re-layouts: 6.03 us -> 1.67 us
    unnamed x7 -> x3, local copies, waits for them, and re-layouts: 6.03 us -> 1.67 us
where the time goes in v2:
time: 131 us
  Pallas kernels  128 us (98%)
  local copies, waits for them, and re-layouts  1.67 us (1%)
    pallas_call x1, Pallas kernels, combine(): pl.pallas_call(combine_kernel, out_shape=jax.ShapeDtypeStruct((batch, dim...  70.7 us
    pallas_call x1, Pallas kernels, project(): pl.pallas_call(qkv_kernel, out_shape=jax.ShapeDtypeStruct((sp, 2 + n_head...  36.2 us
    pallas_call x1, Pallas kernels, attend(): pl.pallas_call(attend_kernel, out_shape=(jax.ShapeDtypeStruct(flat, jnp.b...  21.4 us

profile of v2, /device:TPU:0, one launch (start us, length us, event | category | flops | bytes accessed | tf_op | source)
XLA Modules:
  0.0 130.6 jit_solution(16502071267895295024)
XLA Ops:
  0.6 0.0 copy-start
  0.6 36.2 %qkv_exchange.1 = f32[4,18,96,128]{3,2,1,0:T(8,128)} custom-call(s32[96]{0:T(128)} %len_ref.3, bf16[96,16384]{1,0:T(8,128)(2,1)} %hid_hbm.3, bf16[128,128]{1,0:T(8,128)(2,1)} %bitcast.12, f32[1,64]{1,0:T(1,128)} %bitcast.13, bf16[16384,8192]{1,0:T(8,128)(2,1)} %wq.1, bf16[16384,512]{1,0:T(8,128)(2,1)} %wk.1, bf16[16384,512]{1,0:T(8,128)(2,1)} %wv.1), custom_call_target="tpu_custom_call" | custom-call | flops 7247757312 | bytes 75497472 | tf_op jit(solution)/shard_map/qkv_exchange/pallas_call | solution.py:243
  36.8 0.0 copy-done
  36.8 21.4 %attend_local.1 = (bf16[96,512,128]{2,1,0:T(8,128)(2,1)}, bf16[96,512,128]{2,1,0:T(8,128)(2,1)}, f32[6144,128]{1,0:T(8,128)S(1)}, f32[96,128]{1,0:T(8,128)S(1)}) custom-call(s32[96]{0:T(128)S(1)} %copy-done, bf16[96,512,128]{2,1,0:T(8,128)(2,1)} %bitcast.10, bf16[96,512,128]{2,1,0:T(8,128)(2,1)} %bitcast.11, f32[6912,128]{1,0:T(8,128)} %bitcast.9), custom_call_target="tpu_custom_call" | custom-call | flops 1610612736 | bytes 50331648 | tf_op jit(solution)/shard_map/attend_local/pallas_call | solution.py:380
  58.2 70.7 %combine_project.1 = bf16[96,16384]{1,0:T(8,128)(2,1)S(1)} custom-call(f32[64,96,128]{2,1,0:T(8,128)S(1)} %bitcast.8, f32[96,128]{1,0:T(8,128)S(1)} %get-tuple-element.8.ml_ref, bf16[96,16384]{1,0:T(8,128)(2,1)} %hid_hbm.3, bf16[8192,16384]{1,0:T(8,128)(2,1)} %wo.1), custom_call_target="tpu_custom_call" | custom-call | flops 12884901888 | bytes 134217728 | tf_op jit(solution)/shard_map/combine_project/pallas_call | solution.py:627
  128.9 1.7 %copy.14 = bf16[96,16384]{1,0:T(8,128)(2,1)} copy(bf16[96,16384]{1,0:T(8,128)(2,1)S(1)} %combine_project.1) | data formatting | bytes 6291456
Async XLA Ops:
  0.6 36.2 %copy-start = (s32[96]{0:T(128)S(1)}, s32[96]{0:T(128)}, u32[]{:S(2)}) copy-start(s32[96]{0:T(128)} %len_ref.3) | copy-start | bytes 1156

commit v3 on v2

--- a/solution.py
+++ b/solution.py
@@ -14,15 +14,15 @@
 SLOTS = 16
 MIB = 2 ** 20
 MESH_ID = pl.DeviceIdType.MESH
-SEQS = 8
-RING = 8
-AHEAD = 4
+SEQS = 16
+RING = 4
+AHEAD = 2
 MASKED = -3e38
 SCALE = HEAD ** -0.5
 OUT_K = 8192
 OUT_W = 256
 OUT_SLOTS = 6
-PIECE = 8
+PIECE = 4
 
 
 def rope(vec, cos_full, sin_signed):
@@ -32,7 +32,7 @@
 
 
 def qkv_kernel(len_ref, hid_hbm, gain_ref, freq_ref, wq, wk, wv, out_hbm,
-               hid, normed, gain, trig, wbuf, acc, heads, hid_sem, w_sem, v_sem,
+               hid, normed, gain, trig, wbuf, acc, heads, hid_sem, w_sem,
                x_send, x_recv, d_send, d_recv, f_send, f_recv, out_sem):
     batch, dim = hid.shape
     n_k = dim // KT
@@ -55,11 +55,11 @@
     def rows_of(k):
         return pl.ds(pl.multiple_of(k * KT, KT), KT)
 
-    def kv_copies(t):
-        lanes = pl.ds(pl.multiple_of(s * HEAD, HEAD), HEAD)
-        slot = slot_of(t)
-        return (pltpu.make_async_copy(wk.at[rows_of(t), lanes], wbuf.at[slot, :, pl.ds(0, HEAD)], w_sem.at[slot]),
-                pltpu.make_async_copy(wv.at[rows_of(t), lanes], wbuf.at[slot, :, pl.ds(HEAD, HEAD)], v_sem.at[slot]))
+    is_key = s < 2
+
+    def kv_copy(source, t):
+        lanes = pl.ds(pl.multiple_of(lax.rem(s, 2) * half, half), half)
+        return pltpu.make_async_copy(source.at[rows_of(t), lanes], wbuf.at[slot_of(t), :, pl.ds(0, half)], w_sem.at[slot_of(t)])
 
     def wide_copy(t):
         i = t - t_wide
@@ -82,9 +82,12 @@
 
     hid_copy = pltpu.make_async_copy(hid_hbm, hid, hid_sem)
     hid_copy.start()
-    for t in range(n_k):
-        for cp in kv_copies(t):
-            cp.start(priority=1)
+    for mine, source in ((is_key, wk), (jnp.logical_not(is_key), wv)):
+        @pl.when(mine)
+        def _():
+            for t in range(n_k):
+                kv_copy(source, t).start(priority=1)
+
     for t in range(n_k, SLOTS):
         wide_copy(t).start(priority=1)
 
@@ -155,16 +158,16 @@
             acc[:, pl.ds(0, width)] += part
 
     def kv_step(t, carry):
-        for cp in kv_copies(t):
-            cp.wait()
+        kv_copy(wk, t).wait()
         multiply(t, t, half)
         start_tile(t + SLOTS)
         return carry
 
     lax.fori_loop(0, n_k, kv_step, 0)
     pl.semaphore_wait(barrier, 2)
-    heads[s, 0] = rope(acc[:, :HEAD], trig[0], trig[1])
-    heads[s, 1] = acc[:, HEAD:2 * HEAD].astype(jnp.bfloat16).astype(jnp.float32)
+    for h in range(2):
+        vec = acc[:, h * HEAD:(h + 1) * HEAD]
+        heads[s, h] = jnp.where(is_key, rope(vec, trig[0], trig[1]), vec.astype(jnp.bfloat16).astype(jnp.float32))
     publish(0, *units[0])
 
     def wide_step(i, carry):
@@ -183,7 +186,7 @@
             publish(chunk + 1, first, 4)
 
         for u in range(n_wide - 1):
-            @pl.when(i == (u + 1) * n_k + 3)
+            @pl.when(i == (u + 1) * n_k + (3 if u else -3))
             def _():
                 forward(u)
         return carry
@@ -205,13 +208,13 @@
                 heads[s, first + h] = rope(acc[:, h * HEAD:(h + 1) * HEAD], trig[0], trig[1])
             publish(chunk + n_wide + 1, first, 2)
 
-        for c in range(2):
-            @pl.when(i == c * n_k + 4)
-            def _():
-                forward(n_wide - 1 + c)
+        @pl.when(i == 5)
+        def _():
+            forward(n_wide - 1)
         return carry
 
     lax.fori_loop(0, 2 * n_k, tail_step, 0)
+    forward(n_wide)
     forward(n_wide + 1)
     forward(n_wide + 2)
     f_peer = lax.rem(d_peer + 2, 4)
@@ -253,7 +256,7 @@
             pltpu.VMEM((SLOTS, KT, WIDE), jnp.bfloat16),
             pltpu.VMEM((batch, WIDE), jnp.float32),
             pltpu.VMEM((sp, 2 + n_head, batch, HEAD), jnp.float32),
-            dma, dma((SLOTS,)), dma((SLOTS,)),
+            dma, dma((SLOTS,)),
             dma((n_unit,)), dma((n_unit,)), dma((n_unit,)), dma((n_unit,)), dma((n_unit,)), dma((n_unit,)),
             dma((4,)),
         ],
@@ -301,8 +304,8 @@
     qkv_copy.wait()
 
     def new_rows(offset, b):
-        four = qkv[pl.ds(offset * batch + b, n_kv, stride=n_unit * batch), :]
-        return jnp.concatenate([four] * 4, axis=0).astype(jnp.bfloat16)
+        pairs = [qkv[pl.ds((2 * offset + i) * n_unit * batch + b, 2, stride=batch), :] for i in range(2)]
+        return jnp.concatenate(pairs * 4, axis=0).astype(jnp.bfloat16)
 
     def chunk_step(i, carry):
         r = lax.rem(i, RING)

time: 131 us -> 128 us (0.977)
  Pallas kernels: 128 us -> 125 us
    pallas_call x1, Pallas kernels: 21.4 us -> 19.9 us  [attend(): pl.pallas_call(attend_kernel, out_shape=(jax.ShapeDtypeStruct(flat, jnp.b...]
where the time goes in v3:
time: 128 us; the launch traced here: 127 us
  Pallas kernels  125 us (98%)
  local copies, waits for them, and re-layouts  1.67 us (1%)
    pallas_call x1, Pallas kernels, combine(): pl.pallas_call(combine_kernel, out_shape=jax.ShapeDtypeStruct((batch, dim...  69.7 us
    pallas_call x1, Pallas kernels, project(): pl.pallas_call(qkv_kernel, out_shape=jax.ShapeDtypeStruct((sp, 2 + n_head...  35.5 us
    pallas_call x1, Pallas kernels, attend(): pl.pallas_call(attend_kernel, out_shape=(jax.ShapeDtypeStruct(flat, jnp.b...  19.9 us

profile of v3, /device:TPU:0, one launch (start us, length us, event | category | flops | bytes accessed | tf_op | source)
XLA Modules:
  0.0 127.5 jit_solution(10803625616488988559)
XLA Ops:
  0.6 0.0 copy-start
  0.6 35.5 %qkv_exchange.1 = f32[4,18,96,128]{3,2,1,0:T(8,128)} custom-call(s32[96]{0:T(128)} %len_ref.3, bf16[96,16384]{1,0:T(8,128)(2,1)} %hid_hbm.3, bf16[128,128]{1,0:T(8,128)(2,1)} %bitcast.12, f32[1,64]{1,0:T(1,128)} %bitcast.13, bf16[16384,8192]{1,0:T(8,128)(2,1)} %wq.1, bf16[16384,512]{1,0:T(8,128)(2,1)} %wk.1, bf16[16384,512]{1,0:T(8,128)(2,1)} %wv.1), custom_call_target="tpu_custom_call" | custom-call | flops 7247757312 | bytes 75497472 | tf_op jit(solution)/shard_map/qkv_exchange/pallas_call | solution.py:246
  36.2 0.0 copy-done
  36.2 19.9 %attend_local.1 = (bf16[96,512,128]{2,1,0:T(8,128)(2,1)}, bf16[96,512,128]{2,1,0:T(8,128)(2,1)}, f32[6144,128]{1,0:T(8,128)S(1)}, f32[96,128]{1,0:T(8,128)S(1)}) custom-call(s32[96]{0:T(128)S(1)} %copy-done, bf16[96,512,128]{2,1,0:T(8,128)(2,1)} %bitcast.10, bf16[96,512,128]{2,1,0:T(8,128)(2,1)} %bitcast.11, f32[6912,128]{1,0:T(8,128)} %bitcast.9), custom_call_target="tpu_custom_call" | custom-call | flops 1610612736 | bytes 50331648 | tf_op jit(solution)/shard_map/attend_local/pallas_call | solution.py:383
  56.1 69.7 %combine_project.1 = bf16[96,16384]{1,0:T(8,128)(2,1)S(1)} custom-call(f32[64,96,128]{2,1,0:T(8,128)S(1)} %bitcast.8, f32[96,128]{1,0:T(8,128)S(1)} %get-tuple-element.8.ml_ref, bf16[96,16384]{1,0:T(8,128)(2,1)} %hid_hbm.3, bf16[8192,16384]{1,0:T(8,128)(2,1)} %wo.1), custom_call_target="tpu_custom_call" | custom-call | flops 12884901888 | bytes 134217728 | tf_op jit(solution)/shard_map/combine_project/pallas_call | solution.py:630
  125.8 1.7 %copy.14 = bf16[96,16384]{1,0:T(8,128)(2,1)} copy(bf16[96,16384]{1,0:T(8,128)(2,1)S(1)} %combine_project.1) | data formatting | bytes 6291456
Async XLA Ops:
  0.6 35.5 %copy-start = (s32[96]{0:T(128)S(1)}, s32[96]{0:T(128)}, u32[]{:S(2)}) copy-start(s32[96]{0:T(128)} %len_ref.3) | copy-start | bytes 1156

commit v4 on v3

--- a/solution.py
+++ b/solution.py
@@ -21,7 +21,7 @@
 SCALE = HEAD ** -0.5
 OUT_K = 8192
 OUT_W = 256
-OUT_SLOTS = 6
+OUT_SLOTS = 7
 PIECE = 4
 
 
@@ -402,8 +402,8 @@
 
 
 def combine_kernel(own, ml_ref, hid_hbm, wo, ybf,
-                   other, ml_in, ml_chip, gates, mine, x_out, x_in, d_out, d_in, obf, hid, wbuf,
-                   part, part_in, fin, fin_x, fin_d, fin_f,
+                   other, ml_in, ml_chip, gates, mine, x_out, x_in, d_in, obf, hid, wbuf,
+                   part, part_in, fin_x, fin_d, fin_f,
                    hid_sem, w_sem, ml_send, ml_recv, o_send, o_recv, x_send, x_recv, d_send, d_recv,
                    p_send, p_recv, fx_send, fx_recv, fd_send, fd_recv, ff_send, ff_recv):
     n_head, batch, _ = own.shape
@@ -507,7 +507,7 @@
 
     def d_copy(p):
         part_of = pl.ds(p * PIECE, PIECE)
-        return remote(d_out.at[part_of], d_in.at[part_of], d_send.at[p], d_recv.at[p], d_peer)
+        return remote(mine.at[part_of], d_in.at[part_of], d_send.at[p], d_recv.at[p], d_peer)
 
     def head_lanes(h):
         return pl.ds(pl.multiple_of(h * HEAD, HEAD), HEAD)
@@ -520,7 +520,7 @@
             i = p * PIECE + h
             val = (mine_gate[:, h:h + 1] * mine[i] + in_gate[:, h:h + 1] * x_in[i]).astype(jnp.bfloat16)
             obf[:, head_lanes(c * half + i)] = val
-            d_out[i] = val.astype(jnp.float32)
+            mine[i] = val.astype(jnp.float32)
         d_copy(p).start()
         gates[0] = pltpu.roll(gates[0], HEAD - PIECE, 1)
         gates[1] = pltpu.roll(gates[1], HEAD - PIECE, 1)
@@ -542,10 +542,10 @@
         return remote(part.at[j], part_in.at[j], p_send.at[j], p_recv.at[j], None)
 
     def fx_copy(j):
-        return remote(fin.at[j], fin_x.at[j], fx_send.at[j], fx_recv.at[j], x_peer)
+        return remote(part.at[j], fin_x.at[j], fx_send.at[j], fx_recv.at[j], x_peer)
 
     def fd_copy(j):
-        return remote(fin.at[j], fin_d.at[j], fd_send.at[j], fd_recv.at[j], d_peer)
+        return remote(part.at[j], fin_d.at[j], fd_send.at[j], fd_recv.at[j], d_peer)
 
     def ff_copy(j):
         return remote(fin_x.at[j], fin_f.at[j], ff_send.at[j], ff_recv.at[j], d_peer)
@@ -558,7 +558,8 @@
         lane = pl.ds(pl.multiple_of(j * OUT_W, OUT_W), OUT_W)
         val = (hid[:, lane].astype(jnp.float32) + (part[j] + part_in[j])).astype(jnp.bfloat16)
         ybf[my_rows, lanes_of(j, c)] = val
-        fin[j] = val.astype(jnp.float32)
+        p_copy(j).wait_send()
+        part[j] = val.astype(jnp.float32)
         fx_copy(j).start()
         fd_copy(j).start()
 
@@ -605,7 +606,6 @@
         d_copy(p).wait_send()
 
     def drain(j, carry):
-        p_copy(j).wait_send()
         fx_copy(j).wait_send()
         fd_copy(j).wait_send()
         ff_copy(j).wait_send()
@@ -635,10 +635,10 @@
         scratch_shapes=[
             pltpu.VMEM((half, batch, HEAD), f32),
             pltpu.VMEM((2, batch, HEAD), f32), pltpu.VMEM((batch, HEAD), f32), pltpu.VMEM((2, batch, HEAD), f32),
-            quad, quad, quad, quad, quad,
+            quad, quad, quad, quad,
             pltpu.VMEM((rows, n_head * HEAD), jnp.bfloat16), pltpu.VMEM((rows, dim // 2), jnp.bfloat16),
             pltpu.VMEM((OUT_SLOTS, OUT_K, OUT_W), jnp.bfloat16),
-            tiles, tiles, tiles, tiles, tiles, tiles,
+            tiles, tiles, tiles, tiles, tiles,
             dma, dma((OUT_SLOTS,)), dma((2,)), dma((2,)),
             dma((n_piece,)), dma((n_piece,)), dma((n_piece,)), dma((n_piece,)), dma((n_piece,)), dma((n_piece,)),
             dma((n_col,)), dma((n_col,)), dma((n_col,)), dma((n_col,)), dma((n_col,)), dma((n_col,)), dma((n_col,)), dma((n_col,)),

time: 128 us -> 126 us (0.984)
  no operation moved by 1% of the time
where the time goes in v4:
time: 126 us
  Pallas kernels  124 us (98%)
  local copies, waits for them, and re-layouts  1.67 us (1%)
    pallas_call x1, Pallas kernels, combine(): pl.pallas_call(combine_kernel, out_shape=jax.ShapeDtypeStruct((batch, dim...  68.5 us
    pallas_call x1, Pallas kernels, project(): pl.pallas_call(qkv_kernel, out_shape=jax.ShapeDtypeStruct((sp, 2 + n_head...  35.5 us
    pallas_call x1, Pallas kernels, attend(): pl.pallas_call(attend_kernel, out_shape=(jax.ShapeDtypeStruct(flat, jnp.b...  19.9 us

profile of v4, /device:TPU:0, one launch (start us, length us, event | category | flops | bytes accessed | tf_op | source)
XLA Modules:
  0.0 126.2 jit_solution(13170568046724097384)
XLA Ops:
  0.6 0.0 copy-start
  0.6 35.5 %qkv_exchange.1 = f32[4,18,96,128]{3,2,1,0:T(8,128)} custom-call(s32[96]{0:T(128)} %len_ref.3, bf16[96,16384]{1,0:T(8,128)(2,1)} %hid_hbm.3, bf16[128,128]{1,0:T(8,128)(2,1)} %bitcast.12, f32[1,64]{1,0:T(1,128)} %bitcast.13, bf16[16384,8192]{1,0:T(8,128)(2,1)} %wq.1, bf16[16384,512]{1,0:T(8,128)(2,1)} %wk.1, bf16[16384,512]{1,0:T(8,128)(2,1)} %wv.1), custom_call_target="tpu_custom_call" | custom-call | flops 7247757312 | bytes 75497472 | tf_op jit(solution)/shard_map/qkv_exchange/pallas_call | solution.py:246
  36.2 0.0 copy-done
  36.2 19.9 %attend_local.1 = (bf16[96,512,128]{2,1,0:T(8,128)(2,1)}, bf16[96,512,128]{2,1,0:T(8,128)(2,1)}, f32[6144,128]{1,0:T(8,128)S(1)}, f32[96,128]{1,0:T(8,128)S(1)}) custom-call(s32[96]{0:T(128)S(1)} %copy-done, bf16[96,512,128]{2,1,0:T(8,128)(2,1)} %bitcast.10, bf16[96,512,128]{2,1,0:T(8,128)(2,1)} %bitcast.11, f32[6912,128]{1,0:T(8,128)} %bitcast.9), custom_call_target="tpu_custom_call" | custom-call | flops 1610612736 | bytes 50331648 | tf_op jit(solution)/shard_map/attend_local/pallas_call | solution.py:383
  56.1 68.5 %combine_project.1 = bf16[96,16384]{1,0:T(8,128)(2,1)S(1)} custom-call(f32[64,96,128]{2,1,0:T(8,128)S(1)} %bitcast.8, f32[96,128]{1,0:T(8,128)S(1)} %get-tuple-element.8.ml_ref, bf16[96,16384]{1,0:T(8,128)(2,1)} %hid_hbm.3, bf16[8192,16384]{1,0:T(8,128)(2,1)} %wo.1), custom_call_target="tpu_custom_call" | custom-call | flops 12884901888 | bytes 134217728 | tf_op jit(solution)/shard_map/combine_project/pallas_call | solution.py:630
  124.6 1.7 %copy.14 = bf16[96,16384]{1,0:T(8,128)(2,1)} copy(bf16[96,16384]{1,0:T(8,128)(2,1)S(1)} %combine_project.1) | data formatting | bytes 6291456
Async XLA Ops:
  0.6 35.5 %copy-start = (s32[96]{0:T(128)S(1)}, s32[96]{0:T(128)}, u32[]{:S(2)}) copy-start(s32[96]{0:T(128)} %len_ref.3) | copy-start | bytes 1156

commit v5 on v4

--- a/solution.py
+++ b/solution.py
@@ -290,10 +290,10 @@
                 pltpu.make_async_copy(vbuf.at[r], v_out.at[seqs], vo_sem.at[r]))
 
     qkv_copy = pltpu.make_async_copy(qkv_hbm, qkv, qkv_sem)
-    qkv_copy.start()
     for i in range(AHEAD):
         for cp in in_copies(i):
             cp.start()
+    qkv_copy.start()
 
     row = lax.broadcasted_iota(jnp.int32, (n_head, rows), 0)
     col = lax.broadcasted_iota(jnp.int32, (n_head, rows), 1)

time: 126 us -> 128 us (1.016)
  no operation moved by 1% of the time
where the time goes in v5:
time: 128 us; the launch traced here: 127 us
  Pallas kernels  125 us (98%)
  local copies, waits for them, and re-layouts  1.67 us (1%)
    pallas_call x1, Pallas kernels, combine(): pl.pallas_call(combine_kernel, out_shape=jax.ShapeDtypeStruct((batch, dim...  68.4 us
    pallas_call x1, Pallas kernels, project(): pl.pallas_call(qkv_kernel, out_shape=jax.ShapeDtypeStruct((sp, 2 + n_head...  35.5 us
    pallas_call x1, Pallas kernels, attend(): pl.pallas_call(attend_kernel, out_shape=(jax.ShapeDtypeStruct(flat, jnp.b...  21.1 us

profile of v5, /device:TPU:0, one launch (start us, length us, event | category | flops | bytes accessed | tf_op | source)
XLA Modules:
  0.0 127.4 jit_solution(933377519889556979)
XLA Ops:
  0.6 0.0 copy-start
  0.6 35.5 %qkv_exchange.1 = f32[4,18,96,128]{3,2,1,0:T(8,128)} custom-call(s32[96]{0:T(128)} %len_ref.3, bf16[96,16384]{1,0:T(8,128)(2,1)} %hid_hbm.3, bf16[128,128]{1,0:T(8,128)(2,1)} %bitcast.12, f32[1,64]{1,0:T(1,128)} %bitcast.13, bf16[16384,8192]{1,0:T(8,128)(2,1)} %wq.1, bf16[16384,512]{1,0:T(8,128)(2,1)} %wk.1, bf16[16384,512]{1,0:T(8,128)(2,1)} %wv.1), custom_call_target="tpu_custom_call" | custom-call | flops 7247757312 | bytes 75497472 | tf_op jit(solution)/shard_map/qkv_exchange/pallas_call | solution.py:246
  36.2 0.0 copy-done
  36.2 21.1 %attend_local.1 = (bf16[96,512,128]{2,1,0:T(8,128)(2,1)}, bf16[96,512,128]{2,1,0:T(8,128)(2,1)}, f32[6144,128]{1,0:T(8,128)S(1)}, f32[96,128]{1,0:T(8,128)S(1)}) custom-call(s32[96]{0:T(128)S(1)} %copy-done, bf16[96,512,128]{2,1,0:T(8,128)(2,1)} %bitcast.10, bf16[96,512,128]{2,1,0:T(8,128)(2,1)} %bitcast.11, f32[6912,128]{1,0:T(8,128)} %bitcast.9), custom_call_target="tpu_custom_call" | custom-call | flops 1610612736 | bytes 50331648 | tf_op jit(solution)/shard_map/attend_local/pallas_call | solution.py:383
  57.3 68.4 %combine_project.1 = bf16[96,16384]{1,0:T(8,128)(2,1)S(1)} custom-call(f32[64,96,128]{2,1,0:T(8,128)S(1)} %bitcast.8, f32[96,128]{1,0:T(8,128)S(1)} %get-tuple-element.8.ml_ref, bf16[96,16384]{1,0:T(8,128)(2,1)} %hid_hbm.3, bf16[8192,16384]{1,0:T(8,128)(2,1)} %wo.1), custom_call_target="tpu_custom_call" | custom-call | flops 12884901888 | bytes 134217728 | tf_op jit(solution)/shard_map/combine_project/pallas_call | solution.py:630
  125.8 1.7 %copy.14 = bf16[96,16384]{1,0:T(8,128)(2,1)} copy(bf16[96,16384]{1,0:T(8,128)(2,1)S(1)} %combine_project.1) | data formatting | bytes 6291456
Async XLA Ops:
  0.6 35.5 %copy-start = (s32[96]{0:T(128)S(1)}, s32[96]{0:T(128)}, u32[]{:S(2)}) copy-start(s32[96]{0:T(128)} %len_ref.3) | copy-start | bytes 1156
